TPU v7x, 32 devices: a whole 2x2x4 slice. The times are simulated.
32 devices in a mesh: head: 2 (over y), seq: 16 (over z, x, core).
Axes of the slice: x: 2, y: 2, z: 4, core: 2. Of those that a mesh axis runs over, the one named last changes fastest.
Arguments:
- queries: bfloat16 [2048, 4096], P(('seq', 'head')), may hold values from -20 to 20
- keys: bfloat16 [2048, 1024], P(('seq', 'head')), may hold values from -5 to 5
- values: bfloat16 [2048, 1024], P(('seq', 'head')), may hold values from -6 to 6
Outputs:
- attended: bfloat16 [2048, 4096], P(('seq', 'head'))
All inputs are finite; a program needn't handle non-finite values.
Results may differ from a plain program's by a relative error of at most 0.0041.
Values may be sent and summed in bfloat16 or wider, within the bound.
No kernel may reach another device: no remote copies, remote signals or barrier semaphores. Data moves between devices by JAX's collectives and lax.ppermute only.
A program may use at most 64 MiB of HBM per device.

v0:
```python
import math
import jax
import jax.numpy as jnp
from jax import lax
from jax.sharding import PartitionSpec as P

HEAD_DIM = 128


def update_state(state, query_half, query_pos, key_piece, value_piece, key_pos):
    largest, total, summed = state
    score = jnp.einsum("tkgd,pkd->tkgp", query_half, key_piece, preferred_element_type=jnp.float32)
    score = score / math.sqrt(query_half.shape[-1])
    allowed = (key_pos[None, :] <= query_pos[:, None])[:, None, None, :]
    score = jnp.where(allowed, score, jnp.float32(-1e30))
    new_largest = jnp.maximum(largest, jnp.max(score, axis=-1))
    weight = jnp.where(allowed, jnp.exp(score - new_largest[..., None]), jnp.float32(0.0))
    total = jnp.sum(weight, axis=-1)
    product = jnp.einsum(
        "tkgp,pkd->tkgd",
        weight.astype(jnp.bfloat16),
        value_piece,
        preferred_element_type=jnp.float32,
    )
    summed = product
    return (new_largest, total, summed)


def on_device(queries, keys, values):
    q_local, k_local, v_local = (
        lax.all_to_all(queries, "head", split_axis=1, concat_axis=0, tiled=True),
        lax.all_to_all(keys, "head", split_axis=1, concat_axis=0, tiled=True),
        lax.all_to_all(values, "head", split_axis=1, concat_axis=0, tiled=True),
    )
    tokens = q_local.shape[0]
    half = tokens // 2
    kv_local = k_local.shape[1] // HEAD_DIM
    group = q_local.shape[1] // k_local.shape[1]
    index = lax.axis_index("seq")
    offsets = jnp.arange(half, dtype=jnp.int32)
    later = q_local[half:]
    early_pos = index * tokens + offsets
    later_pos = index * tokens + half + offsets
    query_pos = jnp.stack([early_pos, later_pos])
    halves = jnp.stack([q_local[:half], later]).reshape(2, half, kv_local, group, HEAD_DIM)
    start_state = (
        jnp.full((2, half, kv_local, group), -1e30, jnp.float32),
        jnp.zeros((2, half, kv_local, group), jnp.float32),
        jnp.zeros((2, half, kv_local, group, HEAD_DIM), jnp.float32),
    )
    start = jnp.int32(0)
    key_piece = lax.all_gather(k_local, "seq", axis=0, tiled=True)
    value_piece = lax.all_gather(v_local, "seq", axis=0, tiled=True)
    rows = key_piece.shape[0]
    key_piece = key_piece.reshape(rows, kv_local, HEAD_DIM)
    value_piece = value_piece.reshape(rows, kv_local, HEAD_DIM)
    key_pos = jnp.arange(rows, dtype=jnp.int32)
    results = []
    for which in range(2):
        state = (start_state[0][which], start_state[1][which], start_state[2][which])
        needed = start <= query_pos[which, half - 1]

        def run(current, which=which):
            return update_state(
                current, halves[which], query_pos[which], key_piece, value_piece, key_pos
            )

        def keep(current):
            return current

        results.append(lax.cond(needed, run, keep, state))
    total = jnp.stack([results[0][1], results[1][1]])
    summed = jnp.stack([results[0][2], results[1][2]])
    result = (summed / total[..., None]).reshape(2, half, q_local.shape[1]).astype(jnp.bfloat16)
    later_out = result[1]
    combined = jnp.concatenate([result[0], later_out], axis=0)
    return lax.all_to_all(combined, "head", split_axis=0, concat_axis=1, tiled=True)


def solution(mesh):
    return jax.shard_map(
        on_device,
        mesh=mesh,
        in_specs=(P(("seq", "head"), None), P(("seq", "head"), None), P(("seq", "head"), None)),
        out_specs=P(("seq", "head"), None),
        check_vma=False,
    )
```

profile of v0, /device:TPU:0, one launch (start us, length us, event | category | flops | bytes accessed | tf_op | source)
XLA Modules:
  0.0 142.9 jit_solution(106555980706747682)
XLA Ops:
  6.5 0.0 all-gather.3.cloned.1.call-start
  6.5 0.9 copy.81
  7.5 8.6 %all_to_all.73 = bf16[64,2,512]{2,0,1:T(8,128)(2,1)} all-to-all(bf16[64,2,512]{2,0,1:T(8,128)(2,1)S(1)} %bitcast.111), channel_id=1, replica_groups=mesh['head'=2,'seq'=16] {'head'}, dimensions={1} | all-to-all | bytes 262144 | tf_op jit(solution)/shard_map/all_to_all | solution.py:32
  16.1 0.0 all-gather.3.cloned.1.call-update
  16.1 0.0 all-gather.5.cloned.1.call-start
  16.2 0.9 copy.80
  17.1 7.5 %all_to_all.74 = bf16[64,2,512]{2,0,1:T(8,128)(2,1)} all-to-all(bf16[64,2,512]{2,0,1:T(8,128)(2,1)S(1)} %bitcast.112), channel_id=1, replica_groups=mesh['head'=2,'seq'=16] {'head'}, dimensions={1} | all-to-all | bytes 262144 | tf_op jit(solution)/shard_map/all_to_all | solution.py:33
  24.6 0.0 all-gather.5.cloned.1.call-update
  24.6 1.9 %copy.79 = bf16[8,2,8,2048]{3,2,0,1:T(8,128)(2,1)} copy(bf16[8,2,8,2048]{3,2,1,0:T(8,128)(2,1)} %bitcast.108) | data formatting | bytes 1048576 | tf_op jit(solution)/shard_map/all_to_all | solution.py:31
  26.5 3.5 %all-to-all-start = ((bf16[64,2,2048]{2,0,1:T(8,128)(2,1)}), bf16[64,2,2048]{2,0,1:T(8,128)(2,1)S(1)}, u32[]{:S(2)}, u32[]{:S(2)}) async-start(bf16[64,2,2048]{2,0,1:T(8,128)(2,1)} %bitcast.98), calls=%async_computation | async-start | bytes 1048576 | tf_op jit(solution)/shard_map/all_to_all | solution.py:31
  30.0 0.6 slice.29
  31.4 0.6 slice.26
  32.6 4.0 %all-to-all-done = bf16[64,2,2048]{2,0,1:T(8,128)(2,1)S(1)} async-done(((bf16[64,2,2048]{2,0,1:T(8,128)(2,1)}), bf16[64,2,2048]{2,0,1:T(8,128)(2,1)S(1)}, u32[]{:S(2)}, u32[]{:S(2)}) %all-to-all-start) | async-done | bytes 524320 | tf_op jit(solution)/shard_map/all_to_all | solution.py:31
  36.6 0.2 stack.42
  36.8 0.2 stack.41
  37.0 0.1 constant_dynamic-update-slice_fusion.1
  37.1 0.1 constant_dynamic-update-slice_fusion
  37.2 21.2 %all-gather.3.cloned.1.call-done = bf16[2048,512]{1,0:T(8,128)(2,1)} async-done(((bf16[128,512]{1,0:T(8,128)(2,1)}), bf16[2048,512]{1,0:T(8,128)(2,1)}) %all-gather.3.cloned.1.call-update) | async-done | bytes 2097168 | tf_op jit(solution)/shard_map/all_gather | solution.py:52
  58.4 2.9 %copy.49 = bf16[2048,512]{0,1:T(8,128)(2,1)S(1)} copy(bf16[2048,512]{1,0:T(8,128)(2,1)} %all-gather.3.cloned.1.call-done) | data formatting | bytes 4194304 | tf_op jit(solution)/shard_map/all_gather | solution.py:52
  61.3 39.4 %all-gather.5.cloned.1.call-done = bf16[2048,512]{1,0:T(8,128)(2,1)} async-done(((bf16[128,512]{1,0:T(8,128)(2,1)}), bf16[2048,512]{1,0:T(8,128)(2,1)}) %all-gather.5.cloned.1.call-update) | async-done | bytes 2097168 | tf_op jit(solution)/shard_map/all_gather | solution.py:53
  100.7 4.0 %copy.51 = bf16[2048,512]{0,1:T(8,128)(2,1)} copy(bf16[2048,512]{1,0:T(8,128)(2,1)} %all-gather.5.cloned.1.call-done) | data formatting | bytes 4194304 | tf_op jit(solution)/shard_map/all_gather | solution.py:53
  104.7 8.9 %conditional.2 = (f32[1,64,4,4]{1,3,2,0:T(4,128)S(1)}, f32[1,64,2048]{2,1,0:T(8,128)S(1)}) conditional(s32[]{:T(128)} %bitcast.12, () %tuple.29, (s32[2048]{0:T(1024)S(1)}, s32[]{:T(128)}, s32[64]{0:T(128)S(1)}, bf16[2,64,4,4,128]{4,3,2,1,0:T(4,128)(2,1)S(1)}, bf16[2048,4,128]{0,2,1:T(8,128)(2,1)S(1)}, ...), branch_computations={%region_0.0_spmd, %region_1.4_spmd} | conditional | flops 1101134848 | bytes 42238768 | solution.py:71
  104.8 0.1 broadcast_compare_fusion
  104.9 0.1 copy.52
  105.0 0.0 copy-start
  105.1 1.7 %fusion = (f32[64,4,4]{0,2,1:T(4,128)S(1)}, f32[4,2048,64,4]{1,2,3,0:T(8,128)S(1)}) fusion(pred[64,2048]{1,0:T(8,128)(4,1)S(1)} %broadcast_compare_fusion, bf16[2,64,4,4,128]{4,1,3,2,0:T(8,128)(2,1)S(1)} %copy.52, bf16[2048,4,128]{0,2,1:T(8,128)(2,1)S(1)} %get-tuple-element.97), kind=kOutput, calls=%fused_computation.2 | convolution fusion | flops 543161344 | bytes 10883072 | tf_op jit(solution)/shard_map/cond/branch_1_fun/tkgd,pkd->tkgp/dot_general | solution.py:12
  106.7 0.0 copy-done
  106.8 1.9 %fusion.9 = f32[64,4,4,128]{3,0,2,1:T(8,128)S(1)} fusion(bf16[2048,4,128]{0,2,1:T(8,128)(2,1)S(1)} %copy-done, f32[4,2048,64,4]{1,2,3,0:T(8,128)S(1)} %get-tuple-element.106, f32[64,4,4]{0,2,1:T(4,128)S(1)} %broadcast_maximum_fusion, pred[64,2048]{1,0:T(8,128)(4,1)S(1)} %broadcast_compare_fusion), kind=kOutput, calls=%fused_computation.10 | convolution fusion | flops 547356672 | bytes 11145216 | tf_op jit(solution)/shard_map/cond/branch_1_fun/tkgp,pkd->tkgd/dot_general | solution.py:19
  108.7 2.5 %fusion.2 = f32[64,4,4]{0,2,1:T(4,128)S(1)} fusion(f32[4,2048,64,4]{1,2,3,0:T(8,128)S(1)} %get-tuple-element.106, f32[64,4,4]{0,2,1:T(4,128)S(1)} %broadcast_maximum_fusion, pred[64,2048]{1,0:T(8,128)(4,1)S(1)} %broadcast_compare_fusion), kind=kLoop, calls=%fused_computation.4 | loop fusion | flops 10484736 | bytes 8527872 | tf_op jit(solution)/shard_map/cond/branch_1_fun/reduce_sum | solution.py:18
  111.2 1.1 copy.45
  112.4 1.3 stack.31
  113.6 8.0 %conditional.3 = (f32[1,64,4,4]{1,3,2,0:T(4,128)S(1)}, f32[1,64,2048]{2,1,0:T(8,128)}) conditional(s32[]{:T(128)} %bitcast.20, () %tuple.31, (s32[2048]{0:T(1024)S(1)}, s32[]{:T(128)}, s32[64]{0:T(128)S(1)}, bf16[2,64,4,4,128]{4,3,2,1,0:T(4,128)(2,1)S(1)}, bf16[2048,4,128]{0,2,1:T(8,128)(2,1)S(1)}, /*index=5*/bf16[2048,4,128]{0,2,1:T(8,128)(2,1)}) %tuple.56), branch_computations={%region_4.5_spmd, %region_5.8_spmd} | conditional | flops 1101134848 | bytes 42238768 | solution.py:71
  113.8 0.1 broadcast_compare_fusion.1
  114.0 0.1 copy.55
  114.1 0.0 copy-start.1
  114.1 1.7 %fusion.17 = (f32[64,4,4]{0,2,1:T(4,128)S(1)}, f32[4,2048,64,4]{1,2,3,0:T(8,128)S(1)}) fusion(pred[64,2048]{1,0:T(8,128)(4,1)S(1)} %broadcast_compare_fusion.1, bf16[2,64,4,4,128]{4,1,3,2,0:T(8,128)(2,1)S(1)} %copy.55, bf16[2048,4,128]{0,2,1:T(8,128)(2,1)S(1)} %get-tuple-element.103), kind=kOutput, calls=%fused_computation.20 | convolution fusion | flops 543161344 | bytes 10883072 | tf_op jit(solution)/shard_map/cond/branch_1_fun/tkgd,pkd->tkgp/dot_general | solution.py:12
  115.8 0.0 copy-done.1
  115.8 1.9 %fusion.26 = f32[64,4,4,128]{3,0,2,1:T(8,128)S(1)} fusion(bf16[2048,4,128]{0,2,1:T(8,128)(2,1)S(1)} %copy-done.1, f32[4,2048,64,4]{1,2,3,0:T(8,128)S(1)} %get-tuple-element.108, f32[64,4,4]{0,2,1:T(4,128)S(1)} %broadcast_maximum_fusion.1, pred[64,2048]{1,0:T(8,128)(4,1)S(1)} %broadcast_compare_fusion.1), kind=kOutput, calls=%fused_computation.28 | convolution fusion | flops 547356672 | bytes 11145216 | tf_op jit(solution)/shard_map/cond/branch_1_fun/tkgp,pkd->tkgd/dot_general | solution.py:19
  117.8 2.5 %fusion.19 = f32[64,4,4]{0,2,1:T(4,128)S(1)} fusion(f32[4,2048,64,4]{1,2,3,0:T(8,128)S(1)} %get-tuple-element.108, f32[64,4,4]{0,2,1:T(4,128)S(1)} %broadcast_maximum_fusion.1, pred[64,2048]{1,0:T(8,128)(4,1)S(1)} %broadcast_compare_fusion.1), kind=kLoop, calls=%fused_computation.22 | loop fusion | flops 10484736 | bytes 8527872 | tf_op jit(solution)/shard_map/cond/branch_1_fun/reduce_sum | solution.py:18
  120.3 0.3 copy.46
  120.7 1.0 stack.35
  121.7 0.2 copy.58
  121.9 0.6 div.21
  122.5 0.4 div.22
  122.9 1.2 fusion.34
  124.2 11.1 %all_to_all.75 = bf16[2,64,2048]{2,1,0:T(8,128)(2,1)S(1)} all-to-all(bf16[2,64,2048]{2,1,0:T(8,128)(2,1)S(1)} %bitcast.106), channel_id=1, replica_groups=mesh['head'=2,'seq'=16] {'head'}, dimensions={0} | all-to-all | bytes 1048576 | tf_op jit(solution)/shard_map/all_to_all | solution.py:77
  135.2 0.8 copy.75
  (14 shorter events, 0.2 us)
Async XLA Ops:
  6.5 51.8 %all-gather.3.cloned.1.call-start = ((), (), s32[]{:S(2)}) async-start(), calls=%async_computation.4 | async-start | bytes 2228224 | tf_op jit(solution)/shard_map/all_gather | solution.py:52
  16.1 84.6 %all-gather.5.cloned.1.call-start = ((), (), s32[]{:S(2)}) async-start(), calls=%async_computation.5 | async-start | bytes 2228224 | tf_op jit(solution)/shard_map/all_gather | solution.py:53
  26.5 10.1 %all-to-all-start = ((bf16[64,2,2048]{2,0,1:T(8,128)(2,1)}), bf16[64,2,2048]{2,0,1:T(8,128)(2,1)S(1)}, u32[]{:S(2)}, u32[]{:S(2)}) async-start(bf16[64,2,2048]{2,0,1:T(8,128)(2,1)} %bitcast.98), calls=%async_computation | async-start | bytes 1048576 | tf_op jit(solution)/shard_map/all_to_all | solution.py:31
  105.0 1.7 %copy-start = (bf16[2048,4,128]{0,2,1:T(8,128)(2,1)S(1)}, bf16[2048,4,128]{0,2,1:T(8,128)(2,1)}, u32[]{:S(2)}) copy-start(bf16[2048,4,128]{0,2,1:T(8,128)(2,1)} %get-tuple-element.98) | copy-start | bytes 6291460 | tf_op jit(solution)/shard_map/cond
  114.1 1.7 %copy-start.1 = (bf16[2048,4,128]{0,2,1:T(8,128)(2,1)S(1)}, bf16[2048,4,128]{0,2,1:T(8,128)(2,1)}, u32[]{:S(2)}) copy-start(bf16[2048,4,128]{0,2,1:T(8,128)(2,1)} %get-tuple-element.104) | copy-start | bytes 6291460 | tf_op jit(solution)/shard_map/cond
Sparse Core Ops, SparseCore 0:
  16.2 42.0 all-gather.2
  60.5 40.1 all-gather.4
where the time goes:
time: 144 us; the launch traced here: 143 us
  waiting for transfers between devices  64.6 us (45%)
  blocking collectives  27.2 us (19%)
  local copies, waits for them, and re-layouts  18.5 us (13%)
  between operations  14.8 us (10%)
  matrix products  7.21 us (5%)
  other arithmetic  6.63 us (5%)
  starting transfers between devices  3.53 us (2%)
    all_gather x1, waiting for transfers between devices, on_device(): value_piece = lax.all_gather(v_local, 'seq', axis=0, tiled=True)  39.4 us
    all_gather x1, waiting for transfers between devices, on_device(): key_piece = lax.all_gather(k_local, 'seq', axis=0, tiled=True)  21.2 us
    all_to_all x1, blocking collectives, on_device(): lax.all_to_all(combined, 'head', split_axis=0, concat_axis=1, tiled=True)  11.1 us
    all_to_all x1, blocking collectives, on_device(): lax.all_to_all(keys, 'head', split_axis=1, concat_axis=0, tiled=True)  8.64 us
    all_to_all x1, blocking collectives, on_device(): lax.all_to_all(values, 'head', split_axis=1, concat_axis=0, tiled=True)  7.52 us
    reduce_sum x2, other arithmetic, update_state(): total = jnp.sum(weight, axis=-1)  5.08 us
    all_to_all x1, waiting for transfers between devices, on_device(): lax.all_to_all(queries, 'head', split_axis=1, concat_axis=0, tiled=True)  3.99 us
    all_gather x1, local copies, waits for them, and re-layouts, on_device(): value_piece = lax.all_gather(v_local, 'seq', axis=0, tiled=True)  3.95 us
  transfers between devices with their start and end apart: 3, of which 3 were waited for; matrix products, arithmetic and copies ran while one was open for 5% of the time, Pallas kernels for 0%

commit v1 on v0

--- a/solution.py
+++ b/solution.py
@@ -5,6 +5,12 @@
 from jax.sharding import PartitionSpec as P
 
 HEAD_DIM = 128
+
+
+def stacked_exchange(x, mesh_axis, split, join):
+    cells = jnp.split(x, lax.axis_size(mesh_axis), axis=split)
+    got = lax.all_to_all(jnp.stack(cells), mesh_axis, 0, 0)
+    return jnp.concatenate(got, axis=join)
 
 
 def update_state(state, query_half, query_pos, key_piece, value_piece, key_pos):
@@ -29,7 +35,7 @@
 def on_device(queries, keys, values):
     q_local, k_local, v_local = (
         lax.all_to_all(queries, "head", split_axis=1, concat_axis=0, tiled=True),
-        lax.all_to_all(keys, "head", split_axis=1, concat_axis=0, tiled=True),
+        stacked_exchange(keys, "head", 1, 0),
         lax.all_to_all(values, "head", split_axis=1, concat_axis=0, tiled=True),
     )
     tokens = q_local.shape[0]

time: 144 us -> 143 us (level)
    all_gather x1, waiting for transfers between devices: 39.4 us -> 21.2 us  [on_device(): value_piece = lax.all_gather(v_local, 'seq', axis=0, tiled=True)]
    all_gather x1, waiting for transfers between devices: 21.2 us -> 38.4 us  [on_device(): key_piece = lax.all_gather(k_local, 'seq', axis=0, tiled=True)]
  transfers between devices with their start and end apart: 3 -> 3, of which waited for: 3 -> 3; matrix products, arithmetic and copies ran while one was open for 5% -> 6% of each run, Pallas kernels for 0% -> 0%
where the time goes in v1:
time: 143 us; the launch traced here: 142 us
  waiting for transfers between devices  63.8 us (45%)
  blocking collectives  27.2 us (19%)
  local copies, waits for them, and re-layouts  18.4 us (13%)
  between operations  14.7 us (10%)
  matrix products  7.21 us (5%)
  other arithmetic  6.65 us (5%)
  starting transfers between devices  3.53 us (2%)
    all_gather x1, waiting for transfers between devices, on_device(): key_piece = lax.all_gather(k_local, 'seq', axis=0, tiled=True)  38.4 us
    all_gather x1, waiting for transfers between devices, on_device(): value_piece = lax.all_gather(v_local, 'seq', axis=0, tiled=True)  21.2 us
    all_to_all x1, blocking collectives, on_device(): lax.all_to_all(combined, 'head', split_axis=0, concat_axis=1, tiled=True)  11.1 us
    all_to_all x1, blocking collectives, on_device(): lax.all_to_all(values, 'head', split_axis=1, concat_axis=0, tiled=True)  8.64 us
    all_to_all x1, blocking collectives, stacked_exchange(): got = lax.all_to_all(jnp.stack(cells), mesh_axis, 0, 0)  7.52 us
    reduce_sum x2, other arithmetic, update_state(): total = jnp.sum(weight, axis=-1)  5.08 us
    all_to_all x1, waiting for transfers between devices, on_device(): lax.all_to_all(queries, 'head', split_axis=1, concat_axis=0, tiled=True)  4.2 us
    all_gather x1, local copies, waits for them, and re-layouts, on_device(): value_piece = lax.all_gather(v_local, 'seq', axis=0, tiled=True)  3.94 us
  transfers between devices with their start and end apart: 3, of which 3 were waited for; matrix products, arithmetic and copies ran while one was open for 6% of the time, Pallas kernels for 0%

profile of v1, /device:TPU:0, one launch (start us, length us, event | category | flops | bytes accessed | tf_op | source)
XLA Modules:
  0.0 141.9 jit_solution(1181739595264005741)
XLA Ops:
  6.5 0.0 all-gather.5.cloned.1.call-start
  6.5 0.9 copy.75
  7.5 8.6 %all_to_all.59 = bf16[64,2,512]{2,0,1:T(8,128)(2,1)} all-to-all(bf16[64,2,512]{2,0,1:T(8,128)(2,1)S(1)} %bitcast.109), channel_id=1, replica_groups=mesh['head'=2,'seq'=16] {'head'}, dimensions={1} | all-to-all | bytes 262144 | tf_op jit(solution)/shard_map/all_to_all | solution.py:39
  16.1 0.0 all-gather.5.cloned.1.call-update
  16.1 0.0 all-gather.3.cloned.1.call-start
  16.2 0.9 slice_bitcast_fusion.7
  17.1 7.5 %all_to_all.60 = bf16[2,64,512]{2,1,0:T(8,128)(2,1)} all-to-all(bf16[2,64,512]{2,1,0:T(8,128)(2,1)S(1)} %pad_maximum_fusion.1), channel_id=1, replica_groups=mesh['head'=2,'seq'=16] {'head'}, dimensions={0} | all-to-all | bytes 262144 | tf_op jit(solution)/shard_map/all_to_all | solution.py:12
  24.6 0.0 all-gather.3.cloned.1.call-update
  24.6 1.9 %copy.74 = bf16[8,2,8,2048]{3,2,0,1:T(8,128)(2,1)} copy(bf16[8,2,8,2048]{3,2,1,0:T(8,128)(2,1)} %bitcast.106) | data formatting | bytes 1048576 | tf_op jit(solution)/shard_map/all_to_all | solution.py:37
  26.5 3.5 %all-to-all-start = ((bf16[64,2,2048]{2,0,1:T(8,128)(2,1)}), bf16[64,2,2048]{2,0,1:T(8,128)(2,1)S(1)}, u32[]{:S(2)}, u32[]{:S(2)}) async-start(bf16[64,2,2048]{2,0,1:T(8,128)(2,1)} %bitcast.97), calls=%async_computation | async-start | bytes 1048576 | tf_op jit(solution)/shard_map/all_to_all | solution.py:37
  30.0 0.6 slice.29
  31.2 0.6 slice.26
  32.4 4.2 %all-to-all-done = bf16[64,2,2048]{2,0,1:T(8,128)(2,1)S(1)} async-done(((bf16[64,2,2048]{2,0,1:T(8,128)(2,1)}), bf16[64,2,2048]{2,0,1:T(8,128)(2,1)S(1)}, u32[]{:S(2)}, u32[]{:S(2)}) %all-to-all-start) | async-done | bytes 524320 | tf_op jit(solution)/shard_map/all_to_all | solution.py:37
  36.6 0.2 stack.51
  36.8 0.2 stack.50
  37.0 0.1 constant_dynamic-update-slice_fusion.1
  37.1 0.1 constant_dynamic-update-slice_fusion
  37.2 21.2 %all-gather.5.cloned.1.call-done = bf16[2048,512]{1,0:T(8,128)(2,1)} async-done(((bf16[128,512]{1,0:T(8,128)(2,1)}), bf16[2048,512]{1,0:T(8,128)(2,1)}) %all-gather.5.cloned.1.call-update) | async-done | bytes 2097168 | tf_op jit(solution)/shard_map/all_gather | solution.py:59
  58.4 3.9 %copy.48 = bf16[2048,512]{0,1:T(8,128)(2,1)} copy(bf16[2048,512]{1,0:T(8,128)(2,1)} %all-gather.5.cloned.1.call-done) | data formatting | bytes 4194304 | tf_op jit(solution)/shard_map/all_gather | solution.py:59
  62.3 38.4 %all-gather.3.cloned.1.call-done = bf16[2048,512]{1,0:T(8,128)(2,1)} async-done(((bf16[128,512]{1,0:T(8,128)(2,1)}), bf16[2048,512]{1,0:T(8,128)(2,1)}) %all-gather.3.cloned.1.call-update) | async-done | bytes 2097168 | tf_op jit(solution)/shard_map/all_gather | solution.py:58
  100.7 2.9 %copy.46 = bf16[2048,512]{0,1:T(8,128)(2,1)S(1)} copy(bf16[2048,512]{1,0:T(8,128)(2,1)} %all-gather.3.cloned.1.call-done) | data formatting | bytes 4194304 | tf_op jit(solution)/shard_map/all_gather | solution.py:58
  103.7 8.9 %conditional.2 = (f32[1,64,4,4]{1,3,2,0:T(4,128)S(1)}, f32[1,64,2048]{2,1,0:T(8,128)S(1)}) conditional(s32[]{:T(128)} %bitcast.12, () %tuple.29, (s32[2048]{0:T(1024)S(1)}, s32[]{:T(128)}, s32[64]{0:T(128)S(1)}, bf16[2,64,4,4,128]{4,3,2,1,0:T(4,128)(2,1)S(1)}, bf16[2048,4,128]{0,2,1:T(8,128)(2,1)S(1)}, ...), branch_computations={%region_0.0_spmd, %region_1.4_spmd} | conditional | flops 1101134848 | bytes 42238768 | solution.py:77
  103.7 0.1 broadcast_compare_fusion
  103.9 0.1 copy.49
  104.0 0.0 copy-start
  104.0 1.7 %fusion = (f32[64,4,4]{0,2,1:T(4,128)S(1)}, f32[4,2048,64,4]{1,2,3,0:T(8,128)S(1)}) fusion(pred[64,2048]{1,0:T(8,128)(4,1)S(1)} %broadcast_compare_fusion, bf16[2,64,4,4,128]{4,1,3,2,0:T(8,128)(2,1)S(1)} %copy.49, bf16[2048,4,128]{0,2,1:T(8,128)(2,1)S(1)} %get-tuple-element.97), kind=kOutput, calls=%fused_computation.2 | convolution fusion | flops 543161344 | bytes 10883072 | tf_op jit(solution)/shard_map/cond/branch_1_fun/tkgd,pkd->tkgp/dot_general | solution.py:18
  105.7 0.0 copy-done
  105.8 1.9 %fusion.9 = f32[64,4,4,128]{3,0,2,1:T(8,128)S(1)} fusion(bf16[2048,4,128]{0,2,1:T(8,128)(2,1)S(1)} %copy-done, f32[4,2048,64,4]{1,2,3,0:T(8,128)S(1)} %get-tuple-element.106, f32[64,4,4]{0,2,1:T(4,128)S(1)} %broadcast_maximum_fusion, pred[64,2048]{1,0:T(8,128)(4,1)S(1)} %broadcast_compare_fusion), kind=kOutput, calls=%fused_computation.10 | convolution fusion | flops 547356672 | bytes 11145216 | tf_op jit(solution)/shard_map/cond/branch_1_fun/tkgp,pkd->tkgd/dot_general | solution.py:25
  107.7 2.5 %fusion.2 = f32[64,4,4]{0,2,1:T(4,128)S(1)} fusion(f32[4,2048,64,4]{1,2,3,0:T(8,128)S(1)} %get-tuple-element.106, f32[64,4,4]{0,2,1:T(4,128)S(1)} %broadcast_maximum_fusion, pred[64,2048]{1,0:T(8,128)(4,1)S(1)} %broadcast_compare_fusion), kind=kLoop, calls=%fused_computation.4 | loop fusion | flops 10484736 | bytes 8527872 | tf_op jit(solution)/shard_map/cond/branch_1_fun/reduce_sum | solution.py:24
  110.2 1.1 copy.43
  111.4 1.3 stack.37
  112.6 8.0 %conditional.3 = (f32[1,64,4,4]{1,3,2,0:T(4,128)S(1)}, f32[1,64,2048]{2,1,0:T(8,128)}) conditional(s32[]{:T(128)} %bitcast.21, () %tuple.31, (s32[2048]{0:T(1024)S(1)}, s32[]{:T(128)}, s32[64]{0:T(128)S(1)}, bf16[2,64,4,4,128]{4,3,2,1,0:T(4,128)(2,1)S(1)}, bf16[2048,4,128]{0,2,1:T(8,128)(2,1)S(1)}, /*index=5*/bf16[2048,4,128]{0,2,1:T(8,128)(2,1)}) %tuple.57), branch_computations={%region_4.5_spmd, %region_5.8_spmd} | conditional | flops 1101134848 | bytes 42238768 | solution.py:77
  112.8 0.1 broadcast_compare_fusion.1
  113.0 0.1 copy.52
  113.1 0.0 copy-start.1
  113.1 1.7 %fusion.17 = (f32[64,4,4]{0,2,1:T(4,128)S(1)}, f32[4,2048,64,4]{1,2,3,0:T(8,128)S(1)}) fusion(pred[64,2048]{1,0:T(8,128)(4,1)S(1)} %broadcast_compare_fusion.1, bf16[2,64,4,4,128]{4,1,3,2,0:T(8,128)(2,1)S(1)} %copy.52, bf16[2048,4,128]{0,2,1:T(8,128)(2,1)S(1)} %get-tuple-element.103), kind=kOutput, calls=%fused_computation.20 | convolution fusion | flops 543161344 | bytes 10883072 | tf_op jit(solution)/shard_map/cond/branch_1_fun/tkgd,pkd->tkgp/dot_general | solution.py:18
  114.8 0.0 copy-done.1
  114.8 1.9 %fusion.26 = f32[64,4,4,128]{3,0,2,1:T(8,128)S(1)} fusion(bf16[2048,4,128]{0,2,1:T(8,128)(2,1)S(1)} %copy-done.1, f32[4,2048,64,4]{1,2,3,0:T(8,128)S(1)} %get-tuple-element.108, f32[64,4,4]{0,2,1:T(4,128)S(1)} %broadcast_maximum_fusion.1, pred[64,2048]{1,0:T(8,128)(4,1)S(1)} %broadcast_compare_fusion.1), kind=kOutput, calls=%fused_computation.28 | convolution fusion | flops 547356672 | bytes 11145216 | tf_op jit(solution)/shard_map/cond/branch_1_fun/tkgp,pkd->tkgd/dot_general | solution.py:25
  116.8 2.5 %fusion.19 = f32[64,4,4]{0,2,1:T(4,128)S(1)} fusion(f32[4,2048,64,4]{1,2,3,0:T(8,128)S(1)} %get-tuple-element.108, f32[64,4,4]{0,2,1:T(4,128)S(1)} %broadcast_maximum_fusion.1, pred[64,2048]{1,0:T(8,128)(4,1)S(1)} %broadcast_compare_fusion.1), kind=kLoop, calls=%fused_computation.22 | loop fusion | flops 10484736 | bytes 8527872 | tf_op jit(solution)/shard_map/cond/branch_1_fun/reduce_sum | solution.py:24
  119.3 0.3 copy.44
  119.7 1.0 stack.41
  120.7 0.2 copy.55
  120.9 0.6 div.21
  121.5 0.4 div.22
  121.9 1.2 fusion.34
  123.2 11.1 %all_to_all.61 = bf16[2,64,2048]{2,1,0:T(8,128)(2,1)S(1)} all-to-all(bf16[2,64,2048]{2,1,0:T(8,128)(2,1)S(1)} %bitcast.104), channel_id=1, replica_groups=mesh['head'=2,'seq'=16] {'head'}, dimensions={0} | all-to-all | bytes 1048576 | tf_op jit(solution)/shard_map/all_to_all | solution.py:83
  134.2 0.8 copy.71
  (15 shorter events, 0.2 us)
Async XLA Ops:
  6.5 51.8 %all-gather.5.cloned.1.call-start = ((), (), s32[]{:S(2)}) async-start(), calls=%async_computation.5 | async-start | bytes 2228224 | tf_op jit(solution)/shard_map/all_gather | solution.py:59
  16.1 84.6 %all-gather.3.cloned.1.call-start = ((), (), s32[]{:S(2)}) async-start(), calls=%async_computation.4 | async-start | bytes 2228224 | tf_op jit(solution)/shard_map/all_gather | solution.py:58
  26.5 10.1 %all-to-all-start = ((bf16[64,2,2048]{2,0,1:T(8,128)(2,1)}), bf16[64,2,2048]{2,0,1:T(8,128)(2,1)S(1)}, u32[]{:S(2)}, u32[]{:S(2)}) async-start(bf16[64,2,2048]{2,0,1:T(8,128)(2,1)} %bitcast.97), calls=%async_computation | async-start | bytes 1048576 | tf_op jit(solution)/shard_map/all_to_all | solution.py:37
  104.0 1.7 %copy-start = (bf16[2048,4,128]{0,2,1:T(8,128)(2,1)S(1)}, bf16[2048,4,128]{0,2,1:T(8,128)(2,1)}, u32[]{:S(2)}) copy-start(bf16[2048,4,128]{0,2,1:T(8,128)(2,1)} %get-tuple-element.98) | copy-start | bytes 6291460 | tf_op jit(solution)/shard_map/cond
  113.1 1.7 %copy-start.1 = (bf16[2048,4,128]{0,2,1:T(8,128)(2,1)S(1)}, bf16[2048,4,128]{0,2,1:T(8,128)(2,1)}, u32[]{:S(2)}) copy-start(bf16[2048,4,128]{0,2,1:T(8,128)(2,1)} %get-tuple-element.104) | copy-start | bytes 6291460 | tf_op jit(solution)/shard_map/cond
Sparse Core Ops, SparseCore 0:
  16.2 42.0 all-gather.4
  60.5 40.1 all-gather.2
